TPU v7x, 32 devices: a whole 2x2x4 slice. The times are simulated.
32 devices in a mesh: img: 4 (over y, core), proj: 8 (over z, x).
Axes of the slice: x: 2, y: 2, z: 4, core: 2. Of those that a mesh axis runs over, the one named last changes fastest.
Arguments:
- images: bfloat16 [512, 4096], P('img'), may hold values from -48 to 48
- projections: bfloat16 [2560, 4096], P('proj'), may hold values from -6 to 6
- noise_weight: float32 [4096], replicated, may hold values from 0.02 to 0.08
- defocus: float32 [512], P('img'), may hold values from 2 to 8
- orient_count: int32 [512], P('img'), may hold values from 160 to 2560, as said below
- term_limit: int32 [512], P('img'), may hold values from 2048 to 4096
- block_plan: int32 [16], replicated, may hold values from 0 to 15, each once
Outputs:
- reconstruction: bfloat16 [2560, 4096], P('proj', 'img')
- evidence_next: float32 [512], P('img')
Inputs may be any that keep to these rules, and one draw needn't show every extreme that they name: Orientations 0 to orient_count[i] - 1 are the significant ones of image i; some image has all 2560.
All inputs are finite; a program needn't handle non-finite values.
Results may differ from a plain program's by a relative error of at most 0.018.
Values may be sent and summed in bfloat16 or wider, within the bound.
A program may use at most 64 MiB of HBM per device.

v0:
```python
import math
import jax
import jax.numpy as jnp
from jax import lax
from jax.sharding import PartitionSpec as P

F = 4096
BLOCK = 32


def contrast_table(defocus, width):
    frequency = (jnp.arange(width, dtype=jnp.float32) + 1.0) / width
    return jnp.sin(2.0 * math.pi * defocus[:, None] * frequency[None, :] + 0.1)


def image_terms(pixels, noise_weight, defocus, limits):
    width = pixels.shape[1]
    contrast = contrast_table(defocus, width)
    keep_mask = (jnp.arange(width, dtype=jnp.int32)[None, :] < limits[:, None]).astype(jnp.float32)
    values = pixels.astype(jnp.float32)
    weighted = (keep_mask * noise_weight[None, :] * contrast * values).astype(jnp.bfloat16)
    weighted_sq = (keep_mask * noise_weight[None, :] * contrast * contrast).astype(jnp.bfloat16)
    back_images = (keep_mask * contrast * values).astype(jnp.bfloat16)
    return (weighted, weighted_sq, back_images)


def slice_weight_sums(every_post, focus_all, limit_all, start, slice_width, img_count, img_rows):
    term_ids = jnp.arange(slice_width, dtype=jnp.int32) + start
    term_float = term_ids.astype(jnp.float32)
    frequency = (term_float + 1.0) / F
    contrast = jnp.sin(2.0 * math.pi * focus_all[:, None] * frequency[None, :] + 0.1)
    keep_mask = (term_float[None, :] < limit_all[:, None]).astype(jnp.float32)
    rebuilt = (keep_mask * contrast * contrast).astype(jnp.bfloat16)
    rebuilt = rebuilt.reshape(img_count, img_rows, slice_width)
    partial_value = jnp.einsum(
        "jbi,bif->bjf", every_post, rebuilt, preferred_element_type=jnp.float32
    )
    partial_value = lax.optimization_barrier(partial_value.astype(jnp.bfloat16)).astype(jnp.float32)
    return jnp.sum(partial_value, axis=0)


def shards(images, projections, noise_weight, defocus, orient_count, term_limit, block_plan):
    proj_rows = projections.shape[0]
    img_rows = images.shape[0]
    weighted, weighted_sq, back_images = image_terms(images, noise_weight, defocus, term_limit)
    proj_sq = (projections.astype(jnp.float32) * projections.astype(jnp.float32)).astype(
        jnp.bfloat16
    )
    contract = (((1,), (1,)), ((), ()))
    scores = lax.dot_general(projections, weighted, contract, preferred_element_type=jnp.float32)
    scores = scores - 0.5 * lax.dot_general(
        proj_sq, weighted_sq, contract, preferred_element_type=jnp.float32
    )
    orient_ids = lax.axis_index("proj") * proj_rows + jnp.arange(proj_rows, dtype=jnp.int32)
    significant = orient_ids[:, None] < orient_count[None, :]
    local_peak = jnp.max(jnp.where(significant, scores, -1e30), axis=0)
    row_peak = lax.pmax(local_peak, "proj")
    safe = jnp.where(significant, scores, row_peak[None, :])
    local_mass = jnp.sum(jnp.where(significant, jnp.exp(safe - row_peak[None, :]), 0.0), axis=0)
    row_mass = lax.psum(local_mass, "proj")
    log_evidence = row_peak + jnp.log(row_mass)
    posterior = jnp.where(significant, jnp.exp(scores - log_evidence[None, :]), 0.0).astype(
        jnp.bfloat16
    )
    img_count = lax.axis_size("img")
    slice_width = F // img_count
    slice_start = lax.axis_index("img") * slice_width
    limit_float = term_limit.astype(jnp.float32)
    moved_images = lax.all_to_all(back_images, "img", split_axis=1, concat_axis=0, tiled=True)
    every_post = lax.all_gather(posterior, "img", axis=1, tiled=True)
    focus_all, limit_all = (
        lax.all_gather(defocus, "img", axis=0, tiled=True),
        lax.all_gather(limit_float, "img", axis=0, tiled=True),
    )
    every_post = every_post.reshape(proj_rows, img_count, img_rows)
    moved_images = moved_images.reshape(img_count, img_rows, slice_width)
    part_images = jnp.einsum(
        "jbi,bif->bjf", every_post, moved_images, preferred_element_type=jnp.float32
    )
    part_images = lax.optimization_barrier(part_images.astype(jnp.bfloat16)).astype(jnp.float32)
    sum_images = jnp.sum(part_images, axis=0)
    sum_weights = slice_weight_sums(
        every_post, focus_all, limit_all, slice_start, slice_width, img_count, img_rows
    )
    reconstruction = (sum_images / (sum_weights + 1.0)).astype(jnp.bfloat16)
    every_evidence = lax.all_gather(log_evidence, "img", axis=0, tiled=True)
    blocks = every_evidence.reshape(-1, BLOCK)
    local_blocks = img_rows // BLOCK
    slot_ids = lax.axis_index("img") * local_blocks + jnp.arange(local_blocks, dtype=jnp.int32)
    selector = (block_plan[None, :] == slot_ids[:, None]).astype(jnp.float32)
    own_blocks = jnp.dot(selector, blocks, precision=lax.Precision.HIGHEST)
    return (reconstruction, own_blocks.reshape(img_rows))


def solution(mesh):
    placed = (P("img", None), P("proj", None), P(), P("img"), P("img"), P("img"), P())
    return jax.shard_map(
        shards, mesh=mesh, in_specs=placed, out_specs=(P("proj", "img"), P("img")), check_vma=False
    )
```

profile of v0, /device:TPU:0, one launch (start us, length us, event | category | flops | bytes accessed | tf_op | source)
XLA Modules:
  0.0 115.0 jit_solution(12315028204032979167)
XLA Ops:
  0.6 0.0 copy-start.3
  0.7 0.7 broadcast_multiply_fusion.1
  1.3 1.6 %copy.15 = bf16[128,4096]{0,1:T(8,128)(2,1)S(1)} copy(bf16[128,4096]{1,0:T(8,128)(2,1)} %param.7) | data formatting | bytes 2097152 | tf_op args[0]
  2.9 8.5 %fusion.2 = bf16[128,4096]{0,1:T(8,128)(2,1)S(1)} fusion(bf16[128,4096]{0,1:T(8,128)(2,1)S(1)} %copy.15, f32[4096]{0:T(1024)S(1)} %add_multiply_fusion, f32[128]{0:T(128)S(1)} %broadcast_multiply_fusion.1, s32[128]{0:T(128)S(1)} %copy-done.3), kind=kLoop, calls=%fused_computation.8 | loop fusion | flops 3670016 | bytes 2114560 | tf_op jit(solution)/shard_map/convert_element_type | solution.py:23
  11.4 0.0 copy-start.5
  11.4 1.3 %copy.16 = bf16[128,4,1024]{2,0,1:T(8,128)(2,1)} copy(bf16[128,4,1024]{0,2,1:T(8,128)(2,1)S(1)} %bitcast.26) | data formatting | bytes 2097152 | tf_op jit(solution)/shard_map/all_to_all | solution.py:69
  12.7 4.3 %all-to-all-start = ((bf16[128,4,1024]{2,0,1:T(8,128)(2,1)}), bf16[128,4,1024]{2,0,1:T(8,128)(2,1)S(1)}, u32[]{:S(2)}, u32[]{:S(2)}) async-start(bf16[128,4,1024]{2,0,1:T(8,128)(2,1)} %copy.16), calls=%async_computation | async-start | bytes 2097152 | tf_op jit(solution)/shard_map/all_to_all | solution.py:69
  17.0 0.0 copy-start.1
  17.0 0.0 copy-start.4
  17.1 12.5 %convolution_bitcast_fusion = f32[320,128]{1,0:T(8,128)S(1)} fusion(bf16[320,4096]{1,0:T(8,128)(2,1)} %param.8, bf16[128,4096]{0,1:T(8,128)(2,1)S(1)} %copy.15, f32[4096]{0:T(1024)S(1)} %add_multiply_fusion, f32[128]{0:T(128)S(1)} %broadcast_multiply_fusion.1, f32[4096]{0:T(1024)S(1)} %copy-done.5, s32[128]{0:T(128)S(1)} %copy-done.3), kind=kOutput, calls=%fused_computation.19 | convolution fusion | flops 339738624 | bytes 3867648 | tf_op jit(solution)/shard_map/dot_general | solution.py:50
  29.6 0.0 copy-start.6
  29.6 0.0 copy-start.2
  29.6 8.2 %fusion.32 = (f32[128]{0:T(128)S(1)}, f32[320,128]{1,0:T(8,128)S(1)}) fusion(s32[128]{0:T(128)S(1)} %copy-done.1, s32[320]{0:T(512)S(1)} %iota_add_fusion, f32[320,128]{1,0:T(8,128)S(1)} %convolution_bitcast_fusion, f32[4096]{0:T(1024)S(1)} %add_multiply_fusion, f32[128]{0:T(128)S(1)} %broadcast_multiply_fusion.1, f32[4096]{0:T(1024)S(1)} %copy-done.5, ...), kind=kOutput, calls=%fused_computation.47 | convolution fusion | flops 343351168 | bytes 2985216 | tf_op jit(solution)/shard_map/dot_general | solution.py:51
  37.7 22.6 %pmax.7 = f32[128]{0:T(128)S(1)} all-reduce(f32[128]{0:T(128)S(1)} %get-tuple-element.2), channel_id=1, replica_groups=mesh['img'=4,'proj'=8] {'proj'}, use_global_device_ids=true, to_apply=%region_1.2 | all-reduce | flops 128 | bytes 1024 | tf_op jit(solution)/shard_map/pmax | solution.py:57
  60.3 0.1 fusion.35
  60.5 17.1 %psum.7 = f32[128]{0:T(128)S(1)} all-reduce(f32[128]{0:T(128)S(1)} %fusion.35), channel_id=1, replica_groups=mesh['img'=4,'proj'=8] {'proj'}, use_global_device_ids=true, to_apply=%region_3.4 | all-reduce | flops 128 | bytes 1024 | tf_op jit(solution)/shard_map/psum | solution.py:60
  77.6 0.1 fusion.36
  77.7 5.1 %all-gather.2 = f32[4,1,128]{2,1,0:T(1,128)S(1)} all-gather(f32[1,1,128]{2,1,0:T(1,128)S(1)} %bitcast.27), channel_id=1, replica_groups=mesh['img'=4,'proj'=8] {'img'}, dimensions={0}, use_global_device_ids=true | all-gather | bytes 2560 | tf_op jit(solution)/shard_map/all_gather | solution.py:86
  82.8 0.5 broadcast.84
  83.3 0.7 reduce.3
  84.0 0.1 reshape.73
  84.0 0.2 fusion.37
  84.2 0.6 reshape.74
  84.8 5.3 %all-gather = f32[4,1,128]{2,1,0:T(1,128)S(1)} all-gather(f32[1,1,128]{2,1,0:T(1,128)S(1)} %convert_bitcast_fusion), channel_id=1, replica_groups=mesh['img'=4,'proj'=8] {'img'}, dimensions={0}, use_global_device_ids=true | all-gather | bytes 2560 | tf_op jit(solution)/shard_map/all_gather | solution.py:73
  90.1 5.0 %all-gather.1 = f32[4,1,128]{2,1,0:T(1,128)S(1)} all-gather(f32[1,1,128]{2,1,0:T(1,128)S(1)} %bitcast.30), channel_id=1, replica_groups=mesh['img'=4,'proj'=8] {'img'}, dimensions={0}, use_global_device_ids=true | all-gather | bytes 2560 | tf_op jit(solution)/shard_map/all_gather | solution.py:72
  95.2 6.3 %all_gather.12 = bf16[320,512]{1,0:T(8,128)(2,1)S(1)} all-gather(bf16[320,128]{1,0:T(8,128)(2,1)S(1)} %fusion.36), channel_id=1, replica_groups=mesh['img'=4,'proj'=8] {'img'}, dimensions={1}, use_global_device_ids=true | all-gather | bytes 409600 | tf_op jit(solution)/shard_map/all_gather | solution.py:70
  101.5 9.4 %convolution_convert_fusion = bf16[4,320,1024]{2,1,0:T(8,128)(2,1)} fusion(f32[1024]{0:T(1024)S(1)} %add_multiply_fusion.1, f32[4,128]{1,0:T(4,128)S(1)} %bitcast.29, f32[4,128]{1,0:T(4,128)S(1)} %bitcast.28, f32[1024]{0:T(1024)S(1)} %add_convert_fusion, bf16[320,512]{1,0:T(8,128)(2,1)S(1)} %all_gather.12), kind=kOutput, calls=%fused_computation.14 | convolution fusion | flops 340000768 | bytes 2961408 | tf_op jit(solution)/shard_map/jbi,bif->bjf/dot_general | solution.py:35
  110.9 0.0 all-to-all-done
  110.9 0.8 convolution_convert_fusion.1
  111.8 0.9 copy-done
  112.7 1.2 %convert_reduce_fusion = (f32[320,1024]{1,0:T(8,128)S(1)}, f32[320,1024]{1,0:T(8,128)S(1)}) fusion(bf16[4,320,1024]{2,1,0:T(8,128)(2,1)S(1)} %copy-done, bf16[4,320,1024]{2,1,0:T(8,128)(2,1)S(1)} %convolution_convert_fusion.1), kind=kLoop, calls=%fused_computation | loop fusion | flops 4587520 | bytes 7864320 | tf_op jit(solution)/shard_map/reduce_sum | solution.py:39
  113.9 1.1 divide_convert_fusion
  (15 shorter events, 0.1 us)
Async XLA Ops:
  0.6 2.3 %copy-start.3 = (s32[128]{0:T(128)S(1)}, s32[128]{0:T(128)}, u32[]{:S(2)}) copy-start(s32[128]{0:T(128)} %param.12) | copy-start | bytes 1540
  11.4 5.6 %copy-start.5 = (f32[4096]{0:T(1024)S(1)}, f32[4096]{0:T(1024)}, u32[]{:S(2)}) copy-start(f32[4096]{0:T(1024)} %param.9) | copy-start | bytes 49156
  12.7 98.2 %all-to-all-start = ((bf16[128,4,1024]{2,0,1:T(8,128)(2,1)}), bf16[128,4,1024]{2,0,1:T(8,128)(2,1)S(1)}, u32[]{:S(2)}, u32[]{:S(2)}) async-start(bf16[128,4,1024]{2,0,1:T(8,128)(2,1)} %copy.16), calls=%async_computation | async-start | bytes 2097152 | tf_op jit(solution)/shard_map/all_to_all | solution.py:69
  17.0 12.5 %copy-start.1 = (s32[128]{0:T(128)S(1)}, s32[128]{0:T(128)}, u32[]{:S(2)}) copy-start(s32[128]{0:T(128)} %param.11) | copy-start | bytes 1540
  17.0 12.5 %copy-start.4 = (bf16[320,4096]{1,0:T(8,128)(2,1)S(1)}, bf16[320,4096]{1,0:T(8,128)(2,1)}, u32[]{:S(2)}) copy-start(bf16[320,4096]{1,0:T(8,128)(2,1)} %param.8) | copy-start | bytes 7864324
  29.6 54.5 %copy-start.6 = (s32[16]{0:T(128)S(1)}, s32[16]{0:T(128)}, u32[]{:S(2)}) copy-start(s32[16]{0:T(128)} %param.13) | copy-start | bytes 196
  29.6 60.6 %copy-start.2 = (f32[128]{0:T(128)S(1)}, f32[128]{0:T(128)}, u32[]{:S(2)}) copy-start(f32[128]{0:T(128)} %param.10) | copy-start | bytes 1540
  110.9 1.7 %copy-start = (bf16[4,320,1024]{2,1,0:T(8,128)(2,1)S(1)}, bf16[4,320,1024]{2,1,0:T(8,128)(2,1)}, u32[]{:S(2)}) copy-start(bf16[4,320,1024]{2,1,0:T(8,128)(2,1)} %convolution_convert_fusion) | copy-start | bytes 7864324
where the time goes:
time: 115 us
  blocking collectives  61.5 us (53%)
  matrix products  31 us (27%)
  other arithmetic  12.4 us (11%)
  local copies, waits for them, and re-layouts  5.05 us (4%)
  starting transfers between devices  4.26 us (4%)
    pmax x1, blocking collectives, shards(): row_peak = lax.pmax(local_peak, 'proj')  22.6 us
    psum x1, blocking collectives, shards(): row_mass = lax.psum(local_mass, 'proj')  17.1 us
    dot_general x1, matrix products, shards(): lax.dot_general(projections, weighted, contract, preferred_element_type=j...  12.5 us
    dot_general x1, matrix products, slice_weight_sums(): jnp.einsum('jbi,bif->bjf', every_post, rebuilt, preferred_element_type=jn...  9.38 us
    convert_element_type x1, other arithmetic, image_terms(): back_images = (keep_mask * contrast * values).astype(jnp.bfloat16)  8.45 us
    dot_general x1, matrix products, shards(): lax.dot_general(proj_sq, weighted_sq, contract, preferred_element_type=jn...  8.17 us
    all_gather x1, blocking collectives, shards(): every_post = lax.all_gather(posterior, 'img', axis=1, tiled=True)  6.34 us
    all_gather x1, blocking collectives, shards(): lax.all_gather(limit_float, 'img', axis=0, tiled=True)  5.29 us
  transfers between devices with their start and end apart: 1, of which 0 were waited for; matrix products, arithmetic and copies ran while one was open for 28% of the time, Pallas kernels for 0%

commit v1 on v0

--- a/solution.py
+++ b/solution.py
@@ -6,6 +6,25 @@
 
 F = 4096
 BLOCK = 32
+
+
+def in_order(blocks, dim):
+    lengths = list(blocks.shape[1:])
+    lengths[dim] *= blocks.shape[0]
+    return jnp.moveaxis(blocks, 0, dim).reshape(lengths)
+
+
+def collected_by_bits(x, axis):
+    peers, here = (lax.axis_size(axis), lax.axis_index(axis))
+    blocks, apart = (x[None], 1)
+    while apart < peers:
+        partner_block = lax.ppermute(blocks, axis, [(i, i ^ apart) for i in range(peers)])
+        low = here & apart == 0
+        blocks = jnp.concatenate(
+            [jnp.where(low, blocks, partner_block), jnp.where(low, partner_block, blocks)]
+        )
+        apart *= 2
+    return blocks
 
 
 def contrast_table(defocus, width):
@@ -67,7 +86,7 @@
     slice_start = lax.axis_index("img") * slice_width
     limit_float = term_limit.astype(jnp.float32)
     moved_images = lax.all_to_all(back_images, "img", split_axis=1, concat_axis=0, tiled=True)
-    every_post = lax.all_gather(posterior, "img", axis=1, tiled=True)
+    every_post = in_order(collected_by_bits(posterior, "img"), 1)
     focus_all, limit_all = (
         lax.all_gather(defocus, "img", axis=0, tiled=True),
         lax.all_gather(limit_float, "img", axis=0, tiled=True),

time: 115 us -> 111 us (0.965)
  blocking collectives: 61.5 us -> 55.4 us
  starting transfers between devices: 4.26 us -> 5.98 us
    all_gather x1 -> x0, blocking collectives: 6.34 us -> none  [shards(): every_post = lax.all_gather(posterior, 'img', axis=1, tiled=True)]
    ppermute x0 -> x2, starting transfers between devices: none -> 1.72 us  [collected_by_bits(): lax.ppermute(blocks, axis, [(i, i ^ apart) for i in range(peers)])]
  transfers between devices with their start and end apart: 1 -> 3, of which waited for: 0 -> 0; matrix products, arithmetic and copies ran while one was open for 28% -> 29% of each run, Pallas kernels for 0% -> 0%
where the time goes in v1:
time: 111 us
  blocking collectives  55.4 us (50%)
  matrix products  31.3 us (28%)
  other arithmetic  12.5 us (11%)
  starting transfers between devices  5.98 us (5%)
  local copies, waits for them, and re-layouts  5.04 us (5%)
    pmax x1, blocking collectives, shards(): row_peak = lax.pmax(local_peak, 'proj')  22.6 us
    psum x1, blocking collectives, shards(): row_mass = lax.psum(local_mass, 'proj')  17.1 us
    dot_general x1, matrix products, shards(): lax.dot_general(projections, weighted, contract, preferred_element_type=j...  12.5 us
    dot_general x1, matrix products, slice_weight_sums(): jnp.einsum('jbi,bif->bjf', every_post, rebuilt, preferred_element_type=jn...  9.59 us
    convert_element_type x1, other arithmetic, image_terms(): back_images = (keep_mask * contrast * values).astype(jnp.bfloat16)  8.45 us
    dot_general x1, matrix products, shards(): lax.dot_general(proj_sq, weighted_sq, contract, preferred_element_type=jn...  8.17 us
    all_gather x1, blocking collectives, shards(): lax.all_gather(defocus, 'img', axis=0, tiled=True)  5.44 us
    all_gather x1, blocking collectives, shards(): lax.all_gather(limit_float, 'img', axis=0, tiled=True)  5.18 us
  transfers between devices with their start and end apart: 3, of which 0 were waited for; matrix products, arithmetic and copies ran while one was open for 29% of the time, Pallas kernels for 0%

profile of v1, /device:TPU:0, one launch (start us, length us, event | category | flops | bytes accessed | tf_op | source)
XLA Modules:
  0.0 111.0 jit_solution(11227211934711128961)
XLA Ops:
  0.7 0.7 broadcast_multiply_fusion.1
  1.3 1.6 %copy.11 = bf16[128,4096]{0,1:T(8,128)(2,1)S(1)} copy(bf16[128,4096]{1,0:T(8,128)(2,1)} %param.7) | data formatting | bytes 2097152 | tf_op args[0]
  2.9 8.5 %fusion.2 = bf16[128,4096]{0,1:T(8,128)(2,1)S(1)} fusion(bf16[128,4096]{0,1:T(8,128)(2,1)S(1)} %copy.11, f32[4096]{0:T(1024)S(1)} %add_multiply_fusion, f32[128]{0:T(128)S(1)} %broadcast_multiply_fusion.1, s32[128]{0:T(128)S(1)} %copy-done.3), kind=kLoop, calls=%fused_computation.8 | loop fusion | flops 3670016 | bytes 2114560 | tf_op jit(solution)/shard_map/convert_element_type | solution.py:42
  11.4 0.0 copy-start.5
  11.4 1.3 %copy.12 = bf16[128,4,1024]{2,0,1:T(8,128)(2,1)} copy(bf16[128,4,1024]{0,2,1:T(8,128)(2,1)S(1)} %bitcast.22) | data formatting | bytes 2097152 | tf_op jit(solution)/shard_map/all_to_all | solution.py:88
  12.7 4.3 %all-to-all-start = ((bf16[128,4,1024]{2,0,1:T(8,128)(2,1)}), bf16[128,4,1024]{2,0,1:T(8,128)(2,1)S(1)}, u32[]{:S(2)}, u32[]{:S(2)}) async-start(bf16[128,4,1024]{2,0,1:T(8,128)(2,1)} %copy.12), calls=%async_computation | async-start | bytes 2097152 | tf_op jit(solution)/shard_map/all_to_all | solution.py:88
  17.0 0.0 copy-start.1
  17.0 0.0 copy-start.4
  17.0 12.5 %convolution_bitcast_fusion = f32[320,128]{1,0:T(8,128)S(1)} fusion(bf16[320,4096]{1,0:T(8,128)(2,1)} %param.8, bf16[128,4096]{0,1:T(8,128)(2,1)S(1)} %copy.11, f32[4096]{0:T(1024)S(1)} %add_multiply_fusion, f32[128]{0:T(128)S(1)} %broadcast_multiply_fusion.1, f32[4096]{0:T(1024)S(1)} %copy-done.5, s32[128]{0:T(128)S(1)} %copy-done.3), kind=kOutput, calls=%fused_computation.19 | convolution fusion | flops 339738624 | bytes 3867648 | tf_op jit(solution)/shard_map/dot_general | solution.py:69
  29.5 0.0 copy-start.2
  29.6 0.0 copy-start.6
  29.6 8.2 %fusion.28 = (f32[128]{0:T(128)S(1)}, f32[320,128]{1,0:T(8,128)S(1)}) fusion(s32[128]{0:T(128)S(1)} %copy-done.1, s32[320]{0:T(512)S(1)} %iota_add_fusion, f32[320,128]{1,0:T(8,128)S(1)} %convolution_bitcast_fusion, f32[4096]{0:T(1024)S(1)} %add_multiply_fusion, f32[128]{0:T(128)S(1)} %broadcast_multiply_fusion.1, f32[4096]{0:T(1024)S(1)} %copy-done.5, ...), kind=kOutput, calls=%fused_computation.44 | convolution fusion | flops 343351168 | bytes 2985216 | tf_op jit(solution)/shard_map/dot_general | solution.py:70
  37.7 22.6 %pmax.7 = f32[128]{0:T(128)S(1)} all-reduce(f32[128]{0:T(128)S(1)} %get-tuple-element.6), channel_id=1, replica_groups=mesh['img'=4,'proj'=8] {'proj'}, use_global_device_ids=true, to_apply=%region_1.2 | all-reduce | flops 128 | bytes 1024 | tf_op jit(solution)/shard_map/pmax | solution.py:76
  60.3 0.1 fusion.31
  60.4 17.1 %psum.7 = f32[128]{0:T(128)S(1)} all-reduce(f32[128]{0:T(128)S(1)} %fusion.31), channel_id=1, replica_groups=mesh['img'=4,'proj'=8] {'proj'}, use_global_device_ids=true, to_apply=%region_3.4 | all-reduce | flops 128 | bytes 1024 | tf_op jit(solution)/shard_map/psum | solution.py:79
  77.6 0.1 fusion.33
  77.7 0.1 collective-permute-start
  77.8 5.4 %all-gather.1 = f32[4,1,128]{2,1,0:T(1,128)S(1)} all-gather(f32[1,1,128]{2,1,0:T(1,128)S(1)} %bitcast.26), channel_id=1, replica_groups=mesh['img'=4,'proj'=8] {'img'}, dimensions={0}, use_global_device_ids=true | all-gather | bytes 2560 | tf_op jit(solution)/shard_map/all_gather | solution.py:91
  83.3 5.0 %all-gather.2 = f32[4,1,128]{2,1,0:T(1,128)S(1)} all-gather(f32[1,1,128]{2,1,0:T(1,128)S(1)} %bitcast.23), channel_id=1, replica_groups=mesh['img'=4,'proj'=8] {'img'}, dimensions={0}, use_global_device_ids=true | all-gather | bytes 2560 | tf_op jit(solution)/shard_map/all_gather | solution.py:105
  88.3 0.5 broadcast.84
  88.8 0.7 reduce.3
  89.5 0.1 reshape.69
  89.6 0.2 fusion.34
  89.8 0.1 broadcast_select_fusion.3
  89.9 1.6 %collective-permute-start.1 = (bf16[2,320,128]{2,1,0:T(8,128)(2,1)S(1)}, bf16[2,320,128]{2,1,0:T(8,128)(2,1)S(1)}, u32[]{:S(2)}, u32[]{:S(2)}) collective-permute-start(bf16[2,320,128]{2,1,0:T(8,128)(2,1)S(1)} %pad_maximum_fusion), channel_id=1, source_target_pairs={{0,16},{8,24},{16,0},{24,8},{1,17},{9,25},{17,1},{25,9},{2,18},{10... | collective-permute-start | bytes 491528 | tf_op jit(solution)/shard_map/ppermute | solution.py:21
  91.6 0.6 reshape.70
  92.2 5.2 %all-gather = f32[4,1,128]{2,1,0:T(1,128)S(1)} all-gather(f32[1,1,128]{2,1,0:T(1,128)S(1)} %convert_bitcast_fusion), channel_id=1, replica_groups=mesh['img'=4,'proj'=8] {'img'}, dimensions={0}, use_global_device_ids=true | all-gather | bytes 2560 | tf_op jit(solution)/shard_map/all_gather | solution.py:92
  97.4 9.6 %convolution_convert_fusion = bf16[4,320,1024]{2,1,0:T(8,128)(2,1)} fusion(f32[1024]{0:T(1024)S(1)} %add_multiply_fusion.1, f32[4,128]{1,0:T(4,128)S(1)} %bitcast.25, f32[4,128]{1,0:T(4,128)S(1)} %bitcast.24, f32[1024]{0:T(1024)S(1)} %add_convert_fusion, bf16[2,320,128]{2,1,0:T(8,128)(2,1)S(1)} %get-tuple-element.3, ...), kind=kOutput, calls=%fused_computation.14 | convolution fusion | flops 340164608 | bytes 2961408 | tf_op jit(solution)/shard_map/jbi,bif->bjf/dot_general | solution.py:54
  107.0 0.8 convolution_convert_fusion.1
  107.8 0.9 copy-done
  108.7 1.2 %convert_reduce_fusion = (f32[320,1024]{1,0:T(8,128)S(1)}, f32[320,1024]{1,0:T(8,128)S(1)}) fusion(bf16[4,320,1024]{2,1,0:T(8,128)(2,1)S(1)} %copy-done, bf16[4,320,1024]{2,1,0:T(8,128)(2,1)S(1)} %convolution_convert_fusion.1), kind=kLoop, calls=%fused_computation | loop fusion | flops 4587520 | bytes 7864320 | tf_op jit(solution)/shard_map/reduce_sum | solution.py:58
  109.9 1.1 divide_convert_fusion
  (21 shorter events, 0.1 us)
Async XLA Ops:
  0.6 2.3 %copy-start.3 = (s32[128]{0:T(128)S(1)}, s32[128]{0:T(128)}, u32[]{:S(2)}) copy-start(s32[128]{0:T(128)} %param.12) | copy-start | bytes 1540
  11.4 5.6 %copy-start.5 = (f32[4096]{0:T(1024)S(1)}, f32[4096]{0:T(1024)}, u32[]{:S(2)}) copy-start(f32[4096]{0:T(1024)} %param.9) | copy-start | bytes 49156
  12.7 94.2 %all-to-all-start = ((bf16[128,4,1024]{2,0,1:T(8,128)(2,1)}), bf16[128,4,1024]{2,0,1:T(8,128)(2,1)S(1)}, u32[]{:S(2)}, u32[]{:S(2)}) async-start(bf16[128,4,1024]{2,0,1:T(8,128)(2,1)} %copy.12), calls=%async_computation | async-start | bytes 2097152 | tf_op jit(solution)/shard_map/all_to_all | solution.py:88
  17.0 12.5 %copy-start.1 = (s32[128]{0:T(128)S(1)}, s32[128]{0:T(128)}, u32[]{:S(2)}) copy-start(s32[128]{0:T(128)} %param.11) | copy-start | bytes 1540
  17.0 12.5 %copy-start.4 = (bf16[320,4096]{1,0:T(8,128)(2,1)S(1)}, bf16[320,4096]{1,0:T(8,128)(2,1)}, u32[]{:S(2)}) copy-start(bf16[320,4096]{1,0:T(8,128)(2,1)} %param.8) | copy-start | bytes 7864324
  29.5 48.3 %copy-start.2 = (f32[128]{0:T(128)S(1)}, f32[128]{0:T(128)}, u32[]{:S(2)}) copy-start(f32[128]{0:T(128)} %param.10) | copy-start | bytes 1540
  29.6 60.0 %copy-start.6 = (s32[16]{0:T(128)S(1)}, s32[16]{0:T(128)}, u32[]{:S(2)}) copy-start(s32[16]{0:T(128)} %param.13) | copy-start | bytes 196
  77.7 12.0 %collective-permute-start = (bf16[1,320,128]{2,1,0:T(8,128)(2,1)S(1)}, bf16[1,320,128]{2,1,0:T(8,128)(2,1)S(1)}, u32[]{:S(2)}, u32[]{:S(2)}) collective-permute-start(bf16[1,320,128]{2,1,0:T(8,128)(2,1)S(1)} %fusion.33), channel_id=1, source_target_pairs={{0,8},{8,0},{16,24},{24,16},{1,9},{9,1},{17,25},{25,17},{2,10},{10... | collective-permute-start | bytes 245768 | tf_op jit(solution)/shard_map/ppermute | solution.py:21
  89.9 7.4 %collective-permute-start.1 = (bf16[2,320,128]{2,1,0:T(8,128)(2,1)S(1)}, bf16[2,320,128]{2,1,0:T(8,128)(2,1)S(1)}, u32[]{:S(2)}, u32[]{:S(2)}) collective-permute-start(bf16[2,320,128]{2,1,0:T(8,128)(2,1)S(1)} %pad_maximum_fusion), channel_id=1, source_target_pairs={{0,16},{8,24},{16,0},{24,8},{1,17},{9,25},{17,1},{25,9},{2,18},{10... | collective-permute-start | bytes 491528 | tf_op jit(solution)/shard_map/ppermute | solution.py:21
  107.0 1.7 %copy-start = (bf16[4,320,1024]{2,1,0:T(8,128)(2,1)S(1)}, bf16[4,320,1024]{2,1,0:T(8,128)(2,1)}, u32[]{:S(2)}) copy-start(bf16[4,320,1024]{2,1,0:T(8,128)(2,1)} %convolution_convert_fusion) | copy-start | bytes 7864324
